TPU v7x, 32 devices: a whole 2x2x4 slice. The times are simulated.
32 devices in a mesh: groups: 2 (over x), seq: 16 (over z, y, core).
Axes of the slice: x: 2, y: 2, z: 4, core: 2. Of those that a mesh axis runs over, the one named last changes fastest.
Arguments:
- queries: bfloat16 [4096, 1792], P(('groups', 'seq')), parts along dimension 0, may hold values from -100 to 100
- key_rows: bfloat16 [4096, 256], P(('groups', 'seq')), parts along dimension 0, may hold values from -100 to 100
- value_rows: bfloat16 [4096, 256], P(('groups', 'seq')), parts along dimension 0, may hold values from -6 to 6
- span_order: int32 [64], P('groups'), parts along dimension 0, may hold values from 0 to 31, each once
- kept_blocks: int32 [4, 1], P('groups'), parts along dimension 0, may hold values from 0 to 3, as said below
Outputs:
- attended: bfloat16 [4096, 1792], P(('groups', 'seq')), parts along dimension 0
- kept_cache: bfloat16 [1024, 512], P(('groups', 'seq')), parts along dimension 0
There are 2 independent parts, one for each index of `groups`. A program takes and returns all parts, laid end to end along the dimension named above; each array names one. Nothing has to cross between parts.
Inputs may be any that keep to these rules, and one draw needn't show every extreme that they name: `kept_blocks`: each row lists 1 different blocks.
All inputs are finite; a program needn't handle non-finite values.
Results may differ from a plain program's by a relative error of at most 0.0055.
Values may be sent and summed in bfloat16 or wider, within the bound.
A program may use at most 64 MiB of HBM per device.

v0:
```python
import math
import jax
import jax.numpy as jnp
from jax import lax
from jax.sharding import PartitionSpec as P

HEAD_DIM = 128
BLOCK = 512


def token_positions(span_order, span_len):
    within = jnp.arange(span_len, dtype=jnp.int32)
    return (span_order[:, None] * span_len + within[None, :]).reshape(-1)


def cache_sources(kept_blocks, row_ids):
    block_ids = row_ids // BLOCK
    match = (
        jnp.arange(kept_blocks.shape[1], dtype=jnp.int32)[None, None, :] == block_ids[None, :, None]
    )
    chosen = jnp.sum(jnp.where(match, kept_blocks[:, None, :], 0), axis=-1)
    return chosen * BLOCK + row_ids[None, :] % BLOCK


def local(queries, key_rows, value_rows, span_order, kept_blocks):
    seq_count = lax.axis_size("seq")
    my_index = lax.axis_index("seq")
    query_rows = queries.shape[0]
    kv_heads = key_rows.shape[1] // HEAD_DIM
    group_size = queries.shape[1] // key_rows.shape[1]
    scale = 1.0 / math.sqrt(HEAD_DIM)
    positions = token_positions(span_order, query_rows // 2)
    query_pos = lax.dynamic_slice_in_dim(positions, my_index * query_rows, query_rows)
    query_heads = queries.reshape(query_rows, kv_heads, group_size, HEAD_DIM)
    cache_local = kept_blocks.shape[1] * BLOCK // seq_count
    cache_src = cache_sources(
        kept_blocks, my_index * cache_local + jnp.arange(cache_local, dtype=jnp.int32)
    )

    def pick_rows(sources, key_part, value_part, part_pos):
        onehot = (sources[:, :, None] == part_pos[None, None, :]).astype(jnp.bfloat16)
        count = key_part.shape[0]
        out_rows = sources.shape[1]
        picked_keys = jnp.einsum(
            "hrk,khd->rhd",
            onehot,
            key_part.reshape(count, kv_heads, HEAD_DIM),
            preferred_element_type=jnp.float32,
        )
        picked_values = jnp.einsum(
            "hrk,khd->rhd",
            onehot,
            value_part.reshape(count, kv_heads, HEAD_DIM),
            preferred_element_type=jnp.float32,
        )
        return jnp.concatenate(
            [picked_keys.reshape(out_rows, -1), picked_values.reshape(out_rows, -1)], axis=1
        )

    def attend_block(state, block_keys, block_values, block_pos):
        running_max, totals, accum = (state[0], state[1], state[2])
        count = block_keys.shape[0]
        scores = (
            jnp.einsum(
                "qhgd,khd->hgqk",
                query_heads,
                block_keys.reshape(count, kv_heads, HEAD_DIM),
                preferred_element_type=jnp.float32,
            )
            * scale
        )
        visible = block_pos[None, None, None, :] <= query_pos[None, None, :, None]
        scores = jnp.where(visible, scores, -1e30)
        new_max = jnp.maximum(running_max, jnp.max(scores, axis=-1))
        weights = jnp.where(visible, jnp.exp(scores - new_max[..., None]), 0.0)
        factor = jnp.exp(running_max - new_max)
        totals = totals * factor + jnp.sum(weights, axis=-1)
        mixed = jnp.einsum(
            "hgqk,khd->hgqd",
            weights.astype(jnp.bfloat16),
            block_values.reshape(count, kv_heads, HEAD_DIM),
            preferred_element_type=jnp.float32,
        )
        accum = accum * factor[..., None] + mixed
        return (new_max, totals, accum)

    initial = (
        jnp.full((kv_heads, group_size, query_rows), -1e30, jnp.float32),
        jnp.zeros((kv_heads, group_size, query_rows), jnp.float32),
        jnp.zeros((kv_heads, group_size, query_rows, HEAD_DIM), jnp.float32),
    )
    initial = initial + (jnp.zeros((cache_local, 2 * kv_heads * HEAD_DIM), jnp.float32),)
    piece_keys = lax.all_gather(key_rows, "seq", axis=0, tiled=True)
    piece_values = lax.all_gather(value_rows, "seq", axis=0, tiled=True)
    count = piece_keys.shape[0]
    width = math.gcd(count, 512)

    def inner(step_index, inner_state):
        offset = (step_index * width).astype(jnp.int32)
        block_keys = lax.dynamic_slice_in_dim(piece_keys, offset, width, 0)
        block_values = lax.dynamic_slice_in_dim(piece_values, offset, width, 0)
        block_pos = lax.dynamic_slice_in_dim(positions, offset, width)
        updated = attend_block(inner_state, block_keys, block_values, block_pos)
        extra = (inner_state[3] + pick_rows(cache_src, block_keys, block_values, block_pos),)
        return updated + extra

    final = lax.fori_loop(0, count // width, inner, initial)
    attended = final[2] / final[1][..., None]
    attended = jnp.transpose(attended, (2, 0, 1, 3)).reshape(query_rows, -1).astype(jnp.bfloat16)
    kept_cache = final[3].astype(jnp.bfloat16)
    return (attended, kept_cache)


def solution(mesh):
    placed = (
        P(("groups", "seq"), None),
        P(("groups", "seq"), None),
        P(("groups", "seq"), None),
        P("groups"),
        P("groups", None),
    )
    return jax.shard_map(
        local,
        mesh=mesh,
        in_specs=placed,
        out_specs=(P(("groups", "seq"), None), P(("groups", "seq"), None)),
        check_vma=False,
    )
```

profile of v0, /device:TPU:0, one launch (start us, length us, event | category | flops | bytes accessed | tf_op | source)
XLA Modules:
  0.0 120.7 jit_solution(2158012903326060525)
XLA Ops:
  7.2 0.0 all-gather.3.cloned.1.call-start
  7.2 1.6 %copy.16 = bf16[128,256]{0,1:T(8,128)(2,1)} copy(bf16[128,256]{1,0:T(8,128)(2,1)} %param.8) | data formatting | bytes 131072 | tf_op args[1]
  8.8 0.0 all-gather.3.cloned.1.call-update
  8.8 0.0 all-gather.5.cloned.1.call-start
  8.9 1.6 %copy.18 = bf16[128,256]{0,1:T(8,128)(2,1)} copy(bf16[128,256]{1,0:T(8,128)(2,1)} %param.9) | data formatting | bytes 131072 | tf_op args[2]
  10.4 0.0 all-gather.5.cloned.1.call-update
  10.5 0.7 broadcast_multiply_fusion
  11.2 0.1 iota_add_fusion
  11.2 0.1 add.107
  11.3 1.3 %copy.17 = bf16[128,1792]{0,1:T(8,128)(2,1)S(1)} copy(bf16[128,1792]{1,0:T(8,128)(2,1)} %param.7) | data formatting | bytes 917504 | tf_op args[0]
  12.6 0.3 copy.19
  12.9 0.1 dynamic_slice.24
  13.0 37.1 %all-gather.3.cloned.1.call-done = bf16[2048,256]{0,1:T(8,128)(2,1)} async-done(((bf16[128,256]{0,1:T(8,128)(2,1)}), bf16[2048,256]{0,1:T(8,128)(2,1)}) %all-gather.3.cloned.1.call-update) | async-done | bytes 1048592 | tf_op jit(solution)/shard_map/all_gather | solution.py:93
  50.1 38.4 %all-gather.5.cloned.1.call-done = bf16[2048,256]{0,1:T(8,128)(2,1)} async-done(((bf16[128,256]{0,1:T(8,128)(2,1)}), bf16[2048,256]{0,1:T(8,128)(2,1)}) %all-gather.5.cloned.1.call-update) | async-done | bytes 1048592 | tf_op jit(solution)/shard_map/all_gather | solution.py:94
  88.5 23.3 %while.20 = (s32[]{:T(128)}, f32[2,7,128]{2,1,0:T(8,128)S(1)}, f32[2,7,128]{2,1,0:T(8,128)S(1)}, f32[2,7,128,128]{3,2,1,0:T(8,128)S(1)}, f32[32,512]{1,0:T(8,128...) while((s32[]{:T(128)}, f32[2,7,128]{2,1,0:T(8,128)S(1)}, ...), condition=%wide.region_3.4_spmd.clone, body=%wide.region_0.3_spmd.clone.sunk | while | flops 499344320 | bytes 16182928 | solution.py:107
  88.5 0.7 multiply_add_fusion.2
  89.3 0.1 dynamic_slice.33
  89.3 0.1 broadcast_compare_fusion.2
  89.5 1.1 constant_dynamic-slice_fusion.3
  90.6 0.2 convolution_bitcast_fusion.4
  90.8 0.2 convolution_bitcast_fusion.5
  91.1 0.8 fusion.47
  91.9 0.9 fusion.48
  92.8 1.5 %fusion.50 = f32[2,7,128,128]{3,2,1,0:T(8,128)S(1)} fusion(bf16[512,2,128,1]{0,2,3,1:T(8,128)(2,1)S(1)} %bitcast.80, f32[2,512,128,7]{2,1,3,0:T(8,128)S(1)} %get-tuple-element.372, f32[2,7,128]{2,1,0:T(8,128)S(1)} %select_maximum_fusion.2, pred[128,512]{0,1:T(8,128)(4,1)S(1)} %broadcast_compare_fusion.2, ...), kind=kOutput, calls=%fused_computation.8.clone.1 | convolution fusion | flops 240156672 | bytes 5847041 | tf_op jit(solution)/shard_map/while/body/eval_jaxpr/hgqk,khd->hgqd/dot_general | solution.py:78
  94.4 0.7 multiply_add_fusion.2
  95.1 0.1 dynamic_slice.33
  95.2 0.1 broadcast_compare_fusion.2
  95.3 1.1 constant_dynamic-slice_fusion.3
  96.4 0.2 convolution_bitcast_fusion.4
  96.6 0.2 convolution_bitcast_fusion.5
  96.9 0.8 fusion.47
  97.7 0.9 fusion.48
  98.6 1.5 %fusion.50 = f32[2,7,128,128]{3,2,1,0:T(8,128)S(1)} fusion(bf16[512,2,128,1]{0,2,3,1:T(8,128)(2,1)S(1)} %bitcast.80, f32[2,512,128,7]{2,1,3,0:T(8,128)S(1)} %get-tuple-element.372, f32[2,7,128]{2,1,0:T(8,128)S(1)} %select_maximum_fusion.2, pred[128,512]{0,1:T(8,128)(4,1)S(1)} %broadcast_compare_fusion.2, ...), kind=kOutput, calls=%fused_computation.8.clone.1 | convolution fusion | flops 240156672 | bytes 5847041 | tf_op jit(solution)/shard_map/while/body/eval_jaxpr/hgqk,khd->hgqd/dot_general | solution.py:78
  100.2 0.7 multiply_add_fusion.2
  100.9 0.1 dynamic_slice.33
  101.0 0.1 broadcast_compare_fusion.2
  101.1 1.1 constant_dynamic-slice_fusion.3
  102.2 0.2 convolution_bitcast_fusion.4
  102.4 0.2 convolution_bitcast_fusion.5
  102.7 0.8 fusion.47
  103.5 0.9 fusion.48
  104.4 1.5 %fusion.50 = f32[2,7,128,128]{3,2,1,0:T(8,128)S(1)} fusion(bf16[512,2,128,1]{0,2,3,1:T(8,128)(2,1)S(1)} %bitcast.80, f32[2,512,128,7]{2,1,3,0:T(8,128)S(1)} %get-tuple-element.372, f32[2,7,128]{2,1,0:T(8,128)S(1)} %select_maximum_fusion.2, pred[128,512]{0,1:T(8,128)(4,1)S(1)} %broadcast_compare_fusion.2, ...), kind=kOutput, calls=%fused_computation.8.clone.1 | convolution fusion | flops 240156672 | bytes 5847041 | tf_op jit(solution)/shard_map/while/body/eval_jaxpr/hgqk,khd->hgqd/dot_general | solution.py:78
  106.0 0.7 multiply_add_fusion.2
  106.7 0.1 dynamic_slice.33
  106.8 0.1 broadcast_compare_fusion.2
  106.9 1.1 constant_dynamic-slice_fusion.3
  108.0 0.2 convolution_bitcast_fusion.4
  108.3 0.2 convolution_bitcast_fusion.5
  108.5 0.8 fusion.47
  109.3 0.9 fusion.48
  110.2 1.5 %fusion.50 = f32[2,7,128,128]{3,2,1,0:T(8,128)S(1)} fusion(bf16[512,2,128,1]{0,2,3,1:T(8,128)(2,1)S(1)} %bitcast.80, f32[2,512,128,7]{2,1,3,0:T(8,128)S(1)} %get-tuple-element.372, f32[2,7,128]{2,1,0:T(8,128)S(1)} %select_maximum_fusion.2, pred[128,512]{0,1:T(8,128)(4,1)S(1)} %broadcast_compare_fusion.2, ...), kind=kOutput, calls=%fused_computation.8.clone.1 | convolution fusion | flops 240156672 | bytes 5847041 | tf_op jit(solution)/shard_map/while/body/eval_jaxpr/hgqk,khd->hgqd/dot_general | solution.py:78
  111.8 0.3 copy.20
  112.1 0.1 divide_convert_fusion
  112.2 1.0 copy.21
  113.2 0.6 convert_element_type.25
  (30 shorter events, 0.3 us)
Async XLA Ops:
  7.2 42.9 %all-gather.3.cloned.1.call-start = ((), (), s32[]{:S(2)}) async-start(), calls=%async_computation | async-start | bytes 1114112 | tf_op jit(solution)/shard_map/all_gather | solution.py:93
  8.8 79.7 %all-gather.5.cloned.1.call-start = ((), (), s32[]{:S(2)}) async-start(), calls=%async_computation.1 | async-start | bytes 1114112 | tf_op jit(solution)/shard_map/all_gather | solution.py:94
Sparse Core Ops, SparseCore 0:
  10.7 39.3 all-gather.2
  52.3 36.2 all-gather.4
where the time goes:
time: 121 us
  waiting for transfers between devices  75.6 us (62%)
  between operations  14.1 us (12%)
  matrix products  11 us (9%)
  local copies, waits for them, and re-layouts  10.8 us (9%)
  other arithmetic  8.65 us (7%)
    all_gather x1, waiting for transfers between devices, local(): piece_values = lax.all_gather(value_rows, 'seq', axis=0, tiled=True)  38.4 us
    all_gather x1, waiting for transfers between devices, local(): piece_keys = lax.all_gather(key_rows, 'seq', axis=0, tiled=True)  37.1 us
    dot_general x4, matrix products, attend_block(): jnp.einsum('hgqk,khd->hgqd', weights.astype(jnp.bfloat16), block_values.r...  6.16 us
    unnamed x5, local copies, waits for them, and re-layouts  5.68 us
    dynamic_slice x4, local copies, waits for them, and re-layouts, inner(): block_values = lax.dynamic_slice_in_dim(piece_values, offset, width, 0)  4.29 us
    reduce_sum x4, other arithmetic, attend_block(): totals = totals * factor + jnp.sum(weights, axis=-1)  3.54 us
    dot_general x4, matrix products, attend_block(): jnp.einsum('qhgd,khd->hgqk', query_heads, block_keys.reshape(count, kv_he...  3.13 us
    add x4, other arithmetic, cache_sources(): return chosen * BLOCK + row_ids[None, :] % BLOCK  2.91 us
  transfers between devices with their start and end apart: 2, of which 2 were waited for; matrix products, arithmetic and copies ran while one was open for 3% of the time, Pallas kernels for 0%

commit v1 on v0

--- a/solution.py
+++ b/solution.py
@@ -91,7 +91,9 @@
     )
     initial = initial + (jnp.zeros((cache_local, 2 * kv_heads * HEAD_DIM), jnp.float32),)
     piece_keys = lax.all_gather(key_rows, "seq", axis=0, tiled=True)
-    piece_values = lax.all_gather(value_rows, "seq", axis=0, tiled=True)
+    piece_values = jnp.concatenate(
+        lax.all_to_all(jnp.stack([value_rows] * lax.axis_size("seq")), "seq", 0, 0), axis=0
+    )
     count = piece_keys.shape[0]
     width = math.gcd(count, 512)
 

time: 121 us -> 99.5 us (0.82)
  waiting for transfers between devices: 75.6 us -> 38.9 us
  starting transfers between devices: 0.08 us -> 7.46 us
  other arithmetic: 8.65 us -> 12.4 us
  local copies, waits for them, and re-layouts: 10.8 us -> 14.5 us
    all_gather x1 -> x0, waiting for transfers between devices: 38.4 us -> none  [local(): piece_values = lax.all_gather(value_rows, 'seq', axis=0, tiled=True)]
    all_to_all x0 -> x1, waiting for transfers between devices: none -> 19.2 us  [local(): lax.all_to_all(jnp.stack([value_rows] * lax.axis_size('seq')), 'seq', 0, 0)]
    all_gather x1, waiting for transfers between devices: 37.1 us -> 19.7 us  [local(): piece_keys = lax.all_gather(key_rows, 'seq', axis=0, tiled=True)]
    all_to_all x0 -> x1, starting transfers between devices: none -> 7.41 us  [local(): lax.all_to_all(jnp.stack([value_rows] * lax.axis_size('seq')), 'seq', 0, 0)]
    dynamic_slice x0 -> x4, local copies, waits for them, and re-layouts: none -> 3.9 us  [inner(): block_keys = lax.dynamic_slice_in_dim(piece_keys, offset, width, 0)]
    dynamic_slice x4 -> x8, local copies, waits for them, and re-layouts: 4.29 us -> 0.68 us  [inner(): block_values = lax.dynamic_slice_in_dim(piece_values, offset, width, 0)]
    dynamic_slice x4, local copies, waits for them, and re-layouts: 0.3 us -> 3.04 us  [inner(): block_pos = lax.dynamic_slice_in_dim(positions, offset, width)]
    le x4, other arithmetic: 0.55 us -> 2.92 us  [attend_block(): visible = block_pos[None, None, None, :] <= query_pos[None, None, :, None]]
  transfers between devices with their start and end apart: 2 -> 2, of which waited for: 2 -> 2; matrix products, arithmetic and copies ran while one was open for 3% -> 5% of each run, Pallas kernels for 0% -> 0%
where the time goes in v1:
time: 99.5 us; the launch traced here: 98.9 us
  waiting for transfers between devices  38.9 us (39%)
  local copies, waits for them, and re-layouts  14.5 us (15%)
  between operations  14.1 us (14%)
  other arithmetic  12.4 us (12%)
  matrix products  11.1 us (11%)
  starting transfers between devices  7.46 us (7%)
    all_gather x1, waiting for transfers between devices, local(): piece_keys = lax.all_gather(key_rows, 'seq', axis=0, tiled=True)  19.7 us
    all_to_all x1, waiting for transfers between devices, local(): lax.all_to_all(jnp.stack([value_rows] * lax.axis_size('seq')), 'seq', 0, 0)  19.2 us
    all_to_all x1, starting transfers between devices, local(): lax.all_to_all(jnp.stack([value_rows] * lax.axis_size('seq')), 'seq', 0, 0)  7.41 us
    dot_general x4, matrix products, attend_block(): jnp.einsum('hgqk,khd->hgqd', weights.astype(jnp.bfloat16), block_values.r...  6.21 us
    unnamed x9, local copies, waits for them, and re-layouts  4.11 us
    dynamic_slice x4, local copies, waits for them, and re-layouts, inner(): block_keys = lax.dynamic_slice_in_dim(piece_keys, offset, width, 0)  3.9 us
    reduce_sum x4, other arithmetic, attend_block(): totals = totals * factor + jnp.sum(weights, axis=-1)  3.55 us
    dot_general x4, matrix products, attend_block(): jnp.einsum('qhgd,khd->hgqk', query_heads, block_keys.reshape(count, kv_he...  3.12 us
  transfers between devices with their start and end apart: 2, of which 2 were waited for; matrix products, arithmetic and copies ran while one was open for 5% of the time, Pallas kernels for 0%

profile of v1, /device:TPU:0, one launch (start us, length us, event | category | flops | bytes accessed | tf_op | source)
XLA Modules:
  0.0 98.9 jit_solution(11901568151330493140)
XLA Ops:
  7.2 0.0 copy-start
  7.2 1.0 %copy.44 = bf16[128,256]{0,1:T(8,128)(2,1)S(1)} copy(bf16[128,256]{1,0:T(8,128)(2,1)} %param.9) | data formatting | bytes 131072 | tf_op args[2]
  8.2 1.2 %stack.2 = bf16[16,128,256]{1,2,0:T(8,128)(2,1)} broadcast(bf16[128,256]{0,1:T(8,128)(2,1)S(1)} %copy.44), dimensions={1,2} | broadcast | bytes 1114112 | tf_op jit(solution)/shard_map/stack | solution.py:95
  9.4 7.4 %all-to-all-start = ((bf16[16,128,256]{1,2,0:T(8,128)(2,1)}), bf16[16,128,256]{1,2,0:T(8,128)(2,1)S(1)}, u32[]{:S(2)}, u32[]{:S(2)}) async-start(bf16[16,128,256]{1,2,0:T(8,128)(2,1)} %stack.2), calls=%async_computation | async-start | bytes 2097152 | tf_op jit(solution)/shard_map/all_to_all | solution.py:95
  16.8 0.0 all-gather.2.cloned.1.call-start
  16.9 1.6 %copy.42 = bf16[128,256]{0,1:T(8,128)(2,1)} copy(bf16[128,256]{1,0:T(8,128)(2,1)} %param.8) | data formatting | bytes 131072 | tf_op args[1]
  18.5 0.0 all-gather.2.cloned.1.call-update
  18.5 0.7 broadcast_multiply_fusion
  19.2 0.1 iota_add_fusion
  19.3 0.1 add.107
  19.3 0.0 copy-done
  19.3 0.3 copy.43
  19.6 0.3 copy.46
  19.9 0.6 dynamic_slice.24
  20.5 0.6 and_select_fusion
  21.1 0.6 fusion.21
  21.6 19.2 %all-to-all-done = bf16[16,128,256]{1,2,0:T(8,128)(2,1)S(1)} async-done(((bf16[16,128,256]{1,2,0:T(8,128)(2,1)}), bf16[16,128,256]{1,2,0:T(8,128)(2,1)S(1)}, u32[]{:S(2)}, u32[]{:S(2)}) %all-to-all-start) | async-done | bytes 1048608 | tf_op jit(solution)/shard_map/all_to_all | solution.py:95
  40.9 0.5 copy.45
  41.4 19.7 %all-gather.2.cloned.1.call-done = bf16[2048,256]{0,1:T(8,128)(2,1)} async-done(((bf16[128,256]{0,1:T(8,128)(2,1)}), bf16[2048,256]{0,1:T(8,128)(2,1)}) %all-gather.2.cloned.1.call-update) | async-done | bytes 1048592 | tf_op jit(solution)/shard_map/all_gather | solution.py:93
  61.1 28.9 %while.20 = (s32[]{:T(128)}, f32[2,7,128]{2,1,0:T(8,128)S(1)}, f32[2,7,128]{2,1,0:T(8,128)S(1)}, f32[2,7,128,128]{3,2,1,0:T(8,128)S(1)}, f32[32,512]{1,0:T(8,128...) while((s32[]{:T(128)}, f32[2,7,128]{2,1,0:T(8,128)S(1)}, ...), condition=%wide.region_3.4_spmd.clone, body=%wide.region_0.3_spmd.clone.sunk | while | flops 499344320 | bytes 16707220 | solution.py:109
  61.1 0.8 multiply_add_fusion.2
  61.9 0.8 dynamic_slice.35
  62.6 0.7 broadcast_compare_fusion.2
  63.4 1.0 constant_dynamic-slice_fusion.4
  64.3 0.2 convolution_bitcast_fusion.5
  64.6 0.1 copy.67
  64.8 0.2 convolution_bitcast_fusion.4
  65.0 0.8 fusion.47
  65.8 0.9 fusion.48
  66.7 1.6 %fusion.50 = f32[2,7,128,128]{3,2,1,0:T(8,128)S(1)} fusion(bf16[512,2,128,1]{0,2,3,1:T(8,128)(2,1)S(1)} %bitcast.77, f32[2,512,128,7]{2,1,3,0:T(8,128)S(1)} %get-tuple-element.401, f32[2,7,128]{2,1,0:T(8,128)S(1)} %select_maximum_fusion.2, pred[128,512]{0,1:T(8,128)(4,1)S(1)} %broadcast_compare_fusion.2, ...), kind=kOutput, calls=%fused_computation.8.clone.1 | convolution fusion | flops 240156672 | bytes 5847041 | tf_op jit(solution)/shard_map/while/body/eval_jaxpr/hgqk,khd->hgqd/dot_general | solution.py:78
  68.3 0.8 multiply_add_fusion.2
  69.1 0.8 dynamic_slice.35
  69.9 0.7 broadcast_compare_fusion.2
  70.6 1.0 constant_dynamic-slice_fusion.4
  71.6 0.2 convolution_bitcast_fusion.5
  71.8 0.1 copy.67
  72.0 0.2 convolution_bitcast_fusion.4
  72.2 0.8 fusion.47
  73.0 0.9 fusion.48
  74.0 1.6 %fusion.50 = f32[2,7,128,128]{3,2,1,0:T(8,128)S(1)} fusion(bf16[512,2,128,1]{0,2,3,1:T(8,128)(2,1)S(1)} %bitcast.77, f32[2,512,128,7]{2,1,3,0:T(8,128)S(1)} %get-tuple-element.401, f32[2,7,128]{2,1,0:T(8,128)S(1)} %select_maximum_fusion.2, pred[128,512]{0,1:T(8,128)(4,1)S(1)} %broadcast_compare_fusion.2, ...), kind=kOutput, calls=%fused_computation.8.clone.1 | convolution fusion | flops 240156672 | bytes 5847041 | tf_op jit(solution)/shard_map/while/body/eval_jaxpr/hgqk,khd->hgqd/dot_general | solution.py:78
  75.5 0.8 multiply_add_fusion.2
  76.3 0.8 dynamic_slice.35
  77.1 0.7 broadcast_compare_fusion.2
  77.8 1.0 constant_dynamic-slice_fusion.4
  78.8 0.2 convolution_bitcast_fusion.5
  79.1 0.1 copy.67
  79.2 0.2 convolution_bitcast_fusion.4
  79.5 0.8 fusion.47
  80.3 0.9 fusion.48
  81.2 1.6 %fusion.50 = f32[2,7,128,128]{3,2,1,0:T(8,128)S(1)} fusion(bf16[512,2,128,1]{0,2,3,1:T(8,128)(2,1)S(1)} %bitcast.77, f32[2,512,128,7]{2,1,3,0:T(8,128)S(1)} %get-tuple-element.401, f32[2,7,128]{2,1,0:T(8,128)S(1)} %select_maximum_fusion.2, pred[128,512]{0,1:T(8,128)(4,1)S(1)} %broadcast_compare_fusion.2, ...), kind=kOutput, calls=%fused_computation.8.clone.1 | convolution fusion | flops 240156672 | bytes 5847041 | tf_op jit(solution)/shard_map/while/body/eval_jaxpr/hgqk,khd->hgqd/dot_general | solution.py:78
  82.8 0.8 multiply_add_fusion.2
  83.5 0.8 dynamic_slice.35
  84.3 0.7 broadcast_compare_fusion.2
  85.0 1.0 constant_dynamic-slice_fusion.4
  86.0 0.2 convolution_bitcast_fusion.5
  86.3 0.1 copy.67
  86.4 0.2 convolution_bitcast_fusion.4
  86.7 0.8 fusion.47
  87.5 0.9 fusion.48
  88.4 1.6 %fusion.50 = f32[2,7,128,128]{3,2,1,0:T(8,128)S(1)} fusion(bf16[512,2,128,1]{0,2,3,1:T(8,128)(2,1)S(1)} %bitcast.77, f32[2,512,128,7]{2,1,3,0:T(8,128)S(1)} %get-tuple-element.401, f32[2,7,128]{2,1,0:T(8,128)S(1)} %select_maximum_fusion.2, pred[128,512]{0,1:T(8,128)(4,1)S(1)} %broadcast_compare_fusion.2, ...), kind=kOutput, calls=%fused_computation.8.clone.1 | convolution fusion | flops 240156672 | bytes 5847041 | tf_op jit(solution)/shard_map/while/body/eval_jaxpr/hgqk,khd->hgqd/dot_general | solution.py:78
  90.0 0.3 copy.48
  90.3 0.1 divide_convert_fusion
  90.4 1.0 %copy.49 = bf16[128,1792]{1,0:T(8,128)(2,1)} copy(bf16[128,1792]{0,1:T(8,128)(2,1)S(1)} %bitcast.80) | data formatting | bytes 917504
  91.4 0.6 convert_element_type.25
  (30 shorter events, 0.3 us)
Async XLA Ops:
  7.2 12.2 %copy-start = (bf16[128,1792]{1,0:T(8,128)(2,1)S(1)}, bf16[128,1792]{1,0:T(8,128)(2,1)}, u32[]{:S(2)}) copy-start(bf16[128,1792]{1,0:T(8,128)(2,1)} %param.7) | copy-start | bytes 1376260
  9.4 31.5 %all-to-all-start = ((bf16[16,128,256]{1,2,0:T(8,128)(2,1)}), bf16[16,128,256]{1,2,0:T(8,128)(2,1)S(1)}, u32[]{:S(2)}, u32[]{:S(2)}) async-start(bf16[16,128,256]{1,2,0:T(8,128)(2,1)} %stack.2), calls=%async_computation | async-start | bytes 2097152 | tf_op jit(solution)/shard_map/all_to_all | solution.py:95
  16.8 44.3 %all-gather.2.cloned.1.call-start = ((), (), s32[]{:S(2)}) async-start(), calls=%async_computation.1 | async-start | bytes 1114112 | tf_op jit(solution)/shard_map/all_gather | solution.py:93
  19.3 2.3 %copy-start.1 = (s32[2048]{0:T(1024)}, s32[2048]{0:T(1024)S(1)}, u32[]{:S(2)}) copy-start(s32[2048]{0:T(1024)S(1)} %add.107) | copy-start | bytes 24580
Sparse Core Ops, SparseCore 0:
  20.4 40.6 all-gather.1
